TPU v7x, 32 devices: a whole 2x2x4 slice. The times are simulated.
32 devices in a mesh: dp: 2 (over y), owner: 16 (over z, x, core).
Axes of the slice: x: 2, y: 2, z: 4, core: 2. Of those that a mesh axis runs over, the one named last changes fastest.
Arguments:
- grad_parts: bfloat16 [2, 16, 512, 512], P('dp', None, 'owner'), may hold values from -2.5 to 2.5
- stats: float32 [32, 512, 512], P(('dp', 'owner')), may hold values from -10 to 12, as said below
- roots: bfloat16 [32, 512, 512], P(('dp', 'owner')), may hold values from -0.25 to 0.25
- refresh: int32 [16], P('dp'), may hold values 0 or 1
Outputs:
- new_stats: float32 [32, 512, 512], P(('dp', 'owner'))
- new_roots: bfloat16 [32, 512, 512], P(('dp', 'owner'))
- update: bfloat16 [16, 512, 512], P('dp', 'owner')
Inputs may be any that keep to these rules, and one draw needn't show every extreme that they name: Every stats matrix is symmetric positive definite.
All inputs are finite; a program needn't handle non-finite values. No bound on the sum of `refresh` on one device may be relied on, other than what follows from the above.
Results may differ from a plain program's by a relative error of at most 0.015.
Values may be sent and summed in bfloat16 or wider, within the bound.
No kernel may reach another device: no remote copies, remote signals or barrier semaphores. Data moves between devices by JAX's collectives and lax.ppermute only.
A program may use at most 64 MiB of HBM per device.

v0:
```python
import jax
import jax.numpy as jnp
from jax import lax
from jax.sharding import PartitionSpec as P

ITERS = 5


BETA = 0.8


def partner_2(value, axis, stride):
    mask = 2**stride
    pairs = [(source, source ^ mask) for source in range(lax.axis_size(axis))]
    return lax.ppermute(value, axis, pairs)


def inverse_root(matrix):
    size = matrix.shape[0]
    eye = jnp.eye(size, dtype=jnp.float32)
    scale = jnp.sqrt(jnp.sum(matrix * matrix) + 1e-06)
    current = matrix / scale
    result = eye * scale ** (-0.25)
    for step in range(ITERS):
        factor = (5.0 * eye - current) / 4.0
        result = jnp.dot(result, factor, precision=lax.Precision.HIGHEST)
        if step + 1 < ITERS:
            square = jnp.dot(factor, factor, precision=lax.Precision.HIGHEST)
            fourth = jnp.dot(square, square, precision=lax.Precision.HIGHEST)
            current = jnp.dot(fourth, current, precision=lax.Precision.HIGHEST)
    return result


def local(grad_parts, stats, roots, refresh):
    summed = lax.psum_scatter(grad_parts, "dp", scatter_dimension=1, tiled=True).astype(jnp.float32)
    grad = summed[0].astype(jnp.bfloat16)
    blocks, rows, width = grad.shape
    owner = lax.axis_index("owner")
    side = owner % 2
    flag = lax.dynamic_index_in_dim(refresh, owner // 2, 0, keepdims=False)
    doubled = jnp.repeat(grad, 2, axis=0)
    whole = lax.all_to_all(doubled, "owner", split_axis=0, concat_axis=1, tiled=True)[0]
    oriented = jnp.where(side == 0, whole, whole.T)
    gram = jnp.dot(oriented, oriented.T, preferred_element_type=jnp.float32)
    partner = partner_2(roots, "owner", 0)[0]
    left_root = jnp.where(side == 0, roots[0], partner)
    right_root = jnp.where(side == 0, partner, roots[0])
    product = jnp.dot(left_root, whole, preferred_element_type=jnp.float32).astype(jnp.bfloat16)
    half = width // 2
    right_half = lax.dynamic_slice_in_dim(right_root, side * half, half, 1)
    portion = jnp.dot(product, right_half, preferred_element_type=jnp.float32).astype(jnp.bfloat16)
    moved = lax.all_to_all(portion[None], "owner", split_axis=1, concat_axis=0, tiled=True)
    update = moved.reshape(blocks, 2, rows, half).transpose(0, 2, 1, 3).reshape(blocks, rows, width)
    fresh = BETA * stats[0] + (1.0 - BETA) * (gram / width)
    solved = inverse_root(fresh)
    chosen = jnp.where(flag == 1, solved.astype(jnp.bfloat16), roots[0])
    return (fresh[None], chosen[None], update)


def solution(mesh):
    placed = (
        P("dp", None, "owner", None),
        P(("dp", "owner"), None, None),
        P(("dp", "owner"), None, None),
        P("dp"),
    )
    return jax.shard_map(
        local,
        mesh=mesh,
        in_specs=placed,
        out_specs=(
            P(("dp", "owner"), None, None),
            P(("dp", "owner"), None, None),
            P("dp", "owner", None),
        ),
        check_vma=False,
    )
```

profile of v0, /device:TPU:0, one launch (start us, length us, event | category | flops | bytes accessed | tf_op | source)
XLA Modules:
  0.0 104.2 jit_solution(5590732969121791472)
XLA Ops:
  7.2 0.7 reduce-scatter.2.cloned.1.call-update
  7.9 19.7 %reduce-scatter.2.cloned.1.call-done = bf16[1,8,32,512]{3,2,1,0:T(8,128)(2,1)} async-done(((bf16[1,16,32,512]{3,2,1,0:T(8,128)(2,1)}), bf16[1,8,32,512]{3,2,1,0:T(8,128)(2,1)}) %reduce-scatter.2.cloned.1.call-update) | async-done | bytes 262160 | tf_op jit(solution)/shard_map/reduce_scatter | solution.py:35
  27.6 1.8 %broadcast_in_dim.12 = bf16[8,2,32,512]{3,2,1,0:T(8,128)(2,1)} broadcast(bf16[8,32,512]{2,1,0:T(8,128)(2,1)} %bitcast.60), dimensions={0,2,3} | broadcast | bytes 786432 | tf_op jit(solution)/shard_map/broadcast_in_dim | solution.py:41
  29.4 5.8 %all-to-all-start = ((bf16[16,32,512]{2,1,0:T(8,128)(2,1)}), bf16[16,32,512]{2,1,0:T(8,128)(2,1)S(1)}, u32[]{:S(2)}, u32[]{:S(2)}) async-start(bf16[16,32,512]{2,1,0:T(8,128)(2,1)} %bitcast.2), calls=%async_computation.1 | async-start | bytes 1048576 | tf_op jit(solution)/shard_map/all_to_all | solution.py:42
  35.2 0.4 collective-permute-start
  35.6 0.7 copy-done.2
  36.2 0.6 dynamic_slice.7
  37.5 12.0 %all-to-all-done = bf16[16,32,512]{2,1,0:T(8,128)(2,1)S(1)} async-done(((bf16[16,32,512]{2,1,0:T(8,128)(2,1)}), bf16[16,32,512]{2,1,0:T(8,128)(2,1)S(1)}, u32[]{:S(2)}, u32[]{:S(2)}) %all-to-all-start) | async-done | bytes 524320 | tf_op jit(solution)/shard_map/all_to_all | solution.py:42
  49.7 1.2 %multiply_reduce_fusion = (f32[]{:T(128)}, f32[512,512]{1,0:T(8,128)S(1)}) fusion(bf16[512,512]{1,0:T(8,128)(2,1)S(1)} %bitcast.54, bf16[512,512]{0,1:T(8,128)(2,1)S(1)} %copy.17, pred[]{:T(512)S(6)} %eq.26, f32[1,512,512]{2,1,0:T(8,128)S(1)} %copy-done), kind=kOutput, calls=%fused_computation.21 | convolution fusion | flops 270008320 | bytes 3145733 | tf_op jit(solution)/shard_map/dot_general | solution.py:44
  51.6 1.9 %fusion.6 = bf16[1,512,256]{2,1,0:T(8,128)(2,1)S(1)} fusion(bf16[512,512]{1,0:T(8,128)(2,1)S(1)} %bitcast.55, bf16[1,512,512]{2,1,0:T(8,128)(2,1)} %param.6, bf16[1,512,512]{2,1,0:T(8,128)(2,1)} %collective-permute-done, pred[]{:T(512)S(6)} %eq.26, bf16[512,512]{1,0:T(8,128)(2,1)} %bitcast.7, s32[]{:T(128)S(6)} %select_n.56, bf16[512,512]{1,0:T(8,128)(2,1)} %bitcast.10), kind=kOutput, calls=%fused_computation.14 | convolution fusion | flops 403439616 | bytes 2360832 | tf_op jit(solution)/shard_map/dot_general | solution.py:51
  53.9 0.5 broadcast.126
  54.4 2.2 %reduce = bf16[512,256]{1,0:T(8,128)(2,1)S(1)} reduce(bf16[512,1,256]{2,1,0:T(2,128)(2,1)S(1)} %bitcast.57, bf16[]{:T(256)} %broadcast.126), dimensions={1}, to_apply=%bitcast.52.reduce_sub_computation | reduce | bytes 524290
  56.7 0.8 reshape.32
  57.4 4.4 %all-to-all-start.1 = ((bf16[16,2,4096]{2,1,0:T(2,128)(2,1)}), bf16[16,2,4096]{2,1,0:T(2,128)(2,1)S(1)}, u32[]{:S(2)}, u32[]{:S(2)}) async-start(bf16[16,2,4096]{2,1,0:T(2,128)(2,1)} %reshape.32), calls=%async_computation.2 | async-start | bytes 524288 | tf_op jit(solution)/shard_map/all_to_all | solution.py:52
  61.8 2.0 %fusion.25 = f32[512,512]{1,0:T(8,128)S(1)} fusion(f32[512,512]{1,0:T(8,128)S(1)} %get-tuple-element.4, f32[]{:T(128)S(6)} %sqrt.3), kind=kOutput, calls=%fused_computation.29 | convolution fusion | flops 1611923456 | bytes 2097156 | tf_op jit(solution)/shard_map/dot_general | solution.py:28
  63.8 1.9 %fusion.11 = f32[512,512]{1,0:T(8,128)S(1)} fusion(f32[]{:T(128)S(6)} %pow.3, f32[512,512]{1,0:T(8,128)S(1)} %get-tuple-element.4, f32[]{:T(128)S(6)} %sqrt.3), kind=kOutput, calls=%fused_computation.19 | convolution fusion | flops 1612447744 | bytes 2097160 | tf_op jit(solution)/shard_map/dot_general | solution.py:26
  65.7 1.8 %fusion.88 = f32[512,512]{1,0:T(8,128)S(1)} fusion(f32[512,512]{1,0:T(8,128)S(1)} %fusion.25), kind=kOutput, calls=%fused_computation.91 | convolution fusion | flops 1610612736 | bytes 2097152 | tf_op jit(solution)/shard_map/dot_general | solution.py:29
  67.6 1.9 %fusion.87 = f32[512,512]{1,0:T(8,128)S(1)} fusion(f32[512,512]{1,0:T(8,128)S(1)} %fusion.88, f32[512,512]{1,0:T(8,128)S(1)} %get-tuple-element.4, f32[]{:T(128)S(6)} %sqrt.3), kind=kOutput, calls=%fused_computation.89 | convolution fusion | flops 1610874880 | bytes 3145732 | tf_op jit(solution)/shard_map/dot_general | solution.py:30
  69.5 1.9 %fusion.21 = f32[512,512]{1,0:T(8,128)S(1)} fusion(f32[512,512]{1,0:T(8,128)S(1)} %fusion.87), kind=kOutput, calls=%fused_computation.27 | convolution fusion | flops 1611661312 | bytes 2097152 | tf_op jit(solution)/shard_map/dot_general | solution.py:28
  71.4 1.9 %fusion.23 = f32[512,512]{1,0:T(8,128)S(1)} fusion(f32[512,512]{1,0:T(8,128)S(1)} %fusion.11, f32[512,512]{1,0:T(8,128)S(1)} %fusion.87), kind=kOutput, calls=%fused_computation.28 | convolution fusion | flops 1611661312 | bytes 3145728 | tf_op jit(solution)/shard_map/dot_general | solution.py:26
  73.3 1.8 %fusion.89 = f32[512,512]{1,0:T(8,128)S(1)} fusion(f32[512,512]{1,0:T(8,128)S(1)} %fusion.21), kind=kOutput, calls=%fused_computation.92 | convolution fusion | flops 1610612736 | bytes 2097152 | tf_op jit(solution)/shard_map/dot_general | solution.py:29
  75.2 2.1 %fusion.90 = f32[512,512]{1,0:T(8,128)S(1)} fusion(f32[512,512]{1,0:T(8,128)S(1)} %fusion.89, f32[512,512]{1,0:T(8,128)S(1)} %fusion.87), kind=kOutput, calls=%fused_computation.93 | convolution fusion | flops 1610612736 | bytes 3145728 | tf_op jit(solution)/shard_map/dot_general | solution.py:30
  77.2 1.9 %fusion.17 = f32[512,512]{1,0:T(8,128)S(1)} fusion(f32[512,512]{1,0:T(8,128)S(1)} %fusion.90), kind=kOutput, calls=%fused_computation.25 | convolution fusion | flops 1611661312 | bytes 2097152 | tf_op jit(solution)/shard_map/dot_general | solution.py:28
  79.2 1.9 %fusion.19 = f32[512,512]{1,0:T(8,128)S(1)} fusion(f32[512,512]{1,0:T(8,128)S(1)} %fusion.23, f32[512,512]{1,0:T(8,128)S(1)} %fusion.90), kind=kOutput, calls=%fused_computation.26 | convolution fusion | flops 1611661312 | bytes 3145728 | tf_op jit(solution)/shard_map/dot_general | solution.py:26
  81.1 1.8 %fusion.91 = f32[512,512]{1,0:T(8,128)S(1)} fusion(f32[512,512]{1,0:T(8,128)S(1)} %fusion.17), kind=kOutput, calls=%fused_computation.94 | convolution fusion | flops 1610612736 | bytes 2097152 | tf_op jit(solution)/shard_map/dot_general | solution.py:29
  82.9 1.8 %fusion.92 = f32[512,512]{1,0:T(8,128)S(1)} fusion(f32[512,512]{1,0:T(8,128)S(1)} %fusion.91, f32[512,512]{1,0:T(8,128)S(1)} %fusion.90), kind=kOutput, calls=%fused_computation.95 | convolution fusion | flops 1610612736 | bytes 3145728 | tf_op jit(solution)/shard_map/dot_general | solution.py:30
  84.8 1.9 %fusion.13 = f32[512,512]{1,0:T(8,128)S(1)} fusion(f32[512,512]{1,0:T(8,128)S(1)} %fusion.92), kind=kOutput, calls=%fused_computation.23 | convolution fusion | flops 1611661312 | bytes 2097152 | tf_op jit(solution)/shard_map/dot_general | solution.py:28
  86.7 1.9 %fusion.15 = f32[512,512]{1,0:T(8,128)S(1)} fusion(f32[512,512]{1,0:T(8,128)S(1)} %fusion.19, f32[512,512]{1,0:T(8,128)S(1)} %fusion.92), kind=kOutput, calls=%fused_computation.24 | convolution fusion | flops 1611661312 | bytes 3145728 | tf_op jit(solution)/shard_map/dot_general | solution.py:26
  88.6 2.1 %fusion.93 = f32[512,512]{1,0:T(8,128)S(1)} fusion(f32[512,512]{1,0:T(8,128)S(1)} %fusion.13), kind=kOutput, calls=%fused_computation.96 | convolution fusion | flops 1610612736 | bytes 2097152 | tf_op jit(solution)/shard_map/dot_general | solution.py:29
  90.7 1.8 %fusion.1 = f32[512,512]{1,0:T(8,128)S(1)} fusion(f32[512,512]{1,0:T(8,128)S(1)} %fusion.93, f32[512,512]{1,0:T(8,128)S(1)} %fusion.92), kind=kOutput, calls=%fused_computation.7 | convolution fusion | flops 1611661312 | bytes 3145728 | tf_op jit(solution)/shard_map/dot_general | solution.py:30
  92.6 3.7 %fusion.3 = bf16[1,512,512]{2,1,0:T(8,128)(2,1)} fusion(f32[512,512]{1,0:T(8,128)S(1)} %fusion.15, f32[512,512]{1,0:T(8,128)S(1)} %fusion.1, pred[]{:T(512)} %bitcast.6, bf16[1,512,512]{2,1,0:T(8,128)(2,1)} %param.6), kind=kOutput, calls=%fused_computation.11 | convolution fusion | flops 1611137024 | bytes 3145729 | tf_op jit(solution)/shard_map/dot_general | solution.py:26
  96.6 0.7 copy.21
  (12 shorter events, 1.0 us)
Async XLA Ops:
  7.2 20.4 %reduce-scatter.2.cloned.1.call-start = ((), (), s32[]{:S(2)}) async-start(), calls=%async_computation.3 | async-start | bytes 786432 | tf_op jit(solution)/shard_map/reduce_scatter | solution.py:35
  29.4 20.3 %copy-start = (f32[1,512,512]{2,1,0:T(8,128)S(1)}, f32[1,512,512]{2,1,0:T(8,128)}, u32[]{:S(2)}) copy-start(f32[1,512,512]{2,1,0:T(8,128)} %param.5) | copy-start | bytes 3145732
  29.4 20.0 %all-to-all-start = ((bf16[16,32,512]{2,1,0:T(8,128)(2,1)}), bf16[16,32,512]{2,1,0:T(8,128)(2,1)S(1)}, u32[]{:S(2)}, u32[]{:S(2)}) async-start(bf16[16,32,512]{2,1,0:T(8,128)(2,1)} %bitcast.2), calls=%async_computation.1 | async-start | bytes 1048576 | tf_op jit(solution)/shard_map/all_to_all | solution.py:42
  35.2 16.4 %collective-permute-start = (bf16[1,512,512]{2,1,0:T(8,128)(2,1)}, bf16[1,512,512]{2,1,0:T(8,128)(2,1)}, u32[]{:S(2)}, u32[]{:S(2)}) collective-permute-start(bf16[1,512,512]{2,1,0:T(8,128)(2,1)} %param.6), channel_id=1, source_target_pairs={{0,1},{1,0},{2,3},{3,2},{4,5},{5,4},{6,7},{7,6},{8,9},{9,8},{10,11... | collective-permute-start | bytes 1572872 | tf_op jit(solution)/shard_map/ppermute | solution.py:15
  35.6 0.7 copy-start.2
  50.9 16.7 %copy-start.1 = (f32[512,512]{1,0:T(8,128)}, f32[512,512]{1,0:T(8,128)S(1)}, u32[]{:S(2)}) copy-start(f32[512,512]{1,0:T(8,128)S(1)} %get-tuple-element.4) | copy-start | bytes 3145732
  57.4 38.9 %all-to-all-start.1 = ((bf16[16,2,4096]{2,1,0:T(2,128)(2,1)}), bf16[16,2,4096]{2,1,0:T(2,128)(2,1)S(1)}, u32[]{:S(2)}, u32[]{:S(2)}) async-start(bf16[16,2,4096]{2,1,0:T(2,128)(2,1)} %reshape.32), calls=%async_computation.2 | async-start | bytes 524288 | tf_op jit(solution)/shard_map/all_to_all | solution.py:52
Sparse Core Ops, SparseCore 0:
  10.2 17.3 reduce-scatter.1
where the time goes:
time: 105 us; the launch traced here: 104 us
  matrix products  37.4 us (36%)
  waiting for transfers between devices  32.4 us (31%)
  between operations  15.6 us (15%)
  starting transfers between devices  10.6 us (10%)
  local copies, waits for them, and re-layouts  5.97 us (6%)
  other arithmetic  2.21 us (2%)
    reduce_scatter x1, waiting for transfers between devices, local(): lax.psum_scatter(grad_parts, 'dp', scatter_dimension=1, tiled=True)  19.7 us
    all_to_all x1, waiting for transfers between devices, local(): lax.all_to_all(doubled, 'owner', split_axis=0, concat_axis=1, tiled=True)[0]  12 us
    dot_general x5, matrix products, inverse_root(): result = jnp.dot(result, factor, precision=lax.Precision.HIGHEST)  11.3 us
    dot_general x4, matrix products, inverse_root(): square = jnp.dot(factor, factor, precision=lax.Precision.HIGHEST)  7.72 us
    dot_general x4, matrix products, inverse_root(): current = jnp.dot(fourth, current, precision=lax.Precision.HIGHEST)  7.65 us
    dot_general x4, matrix products, inverse_root(): fourth = jnp.dot(square, square, precision=lax.Precision.HIGHEST)  7.63 us
    all_to_all x1, starting transfers between devices, local(): lax.all_to_all(doubled, 'owner', split_axis=0, concat_axis=1, tiled=True)[0]  5.75 us
    all_to_all x1, starting transfers between devices, local(): lax.all_to_all(portion[None], 'owner', split_axis=1, concat_axis=0, tiled...  4.35 us
  transfers between devices with their start and end apart: 4, of which 2 were waited for; matrix products, arithmetic and copies ran while one was open for 35% of the time, Pallas kernels for 0%

commit v1 on v0

v1 whole, which is shorter than its diff:
```python
import jax
import jax.numpy as jnp
from jax import lax
from jax.experimental import pallas as pl
from jax.experimental.pallas import tpu as pltpu
from jax.sharding import PartitionSpec as P

ITERS = 5
BETA = 0.8


def dot(a, b, dims=((1,), (0,))):
    return lax.dot_general(a, b, (dims, ((), ())), preferred_element_type=jnp.float32)


def product_kernel(core, mine, other, root, partner, whole, portion):
    @pl.when(core[0] == 0)
    def _():
        run_side(0, mine, other, root, partner, whole, portion)

    @pl.when(core[0] == 1)
    def _():
        run_side(1, other, mine, partner, root, whole, portion)


def run_side(side, first, second, left, right, whole, portion):
    chips, rows, width = first.shape
    for chip in range(chips):
        whole[pl.ds(2 * chip * rows, rows), :] = first[chip]
        whole[pl.ds((2 * chip + 1) * rows, rows), :] = second[chip]
    picked = jnp.concatenate(
        [left[pl.ds((2 * chip + side) * rows, rows), :] for chip in range(chips)], axis=0
    )
    product = dot(picked, whole[...]).astype(jnp.bfloat16)
    portion[...] = dot(product, right[...]).astype(jnp.bfloat16)


def root_kernel(flags, whole, stats, root, fresh, chosen, n, y, t, nb, yb):
    width = whole.shape[0]
    weight = (1.0 - BETA) / width

    @pl.when(flags[0] == 0)
    def _():
        fresh[...] = BETA * stats[...] + weight * dot(whole[...], whole[...], ((1,), (1,)))

    @pl.when(flags[0] == 1)
    def _():
        fresh[...] = BETA * stats[...] + weight * dot(whole[...], whole[...], ((0,), (0,)))

    @pl.when(flags[1] == 1)
    def _():
        value = fresh[...]
        total = jnp.sum(jnp.sum(value * value, axis=0, keepdims=True), axis=1, keepdims=True) + 1e-06
        start = value * (0.25 * lax.rsqrt(total))
        n[...] = start
        y[...] = -start
        nb[...] = start.astype(jnp.bfloat16)
        yb[...] = (-start).astype(jnp.bfloat16)

        def square_step():
            t[...] = dot(nb[...], nb[...]) - 2.5 * n[...]
            low = t[...].astype(jnp.bfloat16)
            return (dot(low, low) + 3.125 * t[...]).astype(jnp.bfloat16)

        def advance(grown, first):
            fourth = square_step()
            old = nb[...]
            if not first:
                move = 1.25 * y[...] - grown * n[...] - dot(yb[...], old)
                y[...] = move
                yb[...] = move.astype(jnp.bfloat16)
            new = dot(fourth, old) + 2.44140625 * n[...]
            n[...] = new
            nb[...] = new.astype(jnp.bfloat16)

        advance(1.0, True)

        def body(step, grown):
            advance(grown, False)
            return 1.25 * grown

        grown = lax.fori_loop(1, ITERS - 1, body, jnp.float32(1.25))
        last = 1.25 * y[...] - grown * n[...] - dot(yb[...], nb[...])
        shape = (width, width)
        diagonal = lax.broadcasted_iota(jnp.int32, shape, 0) == lax.broadcasted_iota(jnp.int32, shape, 1)
        scale = lax.rsqrt(jnp.sqrt(jnp.sqrt(total)))
        chosen[...] = ((last + jnp.where(diagonal, 1.25 * grown, 0.0)) * scale).astype(jnp.bfloat16)

    @pl.when(flags[1] != 1)
    def _():
        chosen[...] = root[...]


def local(grad_parts, stats, roots, refresh):
    groups = lax.axis_size("dp")
    owners = lax.axis_size("owner")
    chips = owners // 2
    _, total, rows, width = grad_parts.shape
    blocks = total // groups
    group = lax.axis_index("dp")
    owner = lax.axis_index("owner")
    core = owner % 2
    flag = lax.dynamic_index_in_dim(refresh, owner // 2, 0, keepdims=False)
    swap = [(source, source ^ 1) for source in range(owners)]
    partner = lax.ppermute(roots[0], "owner", swap)

    parts = grad_parts.reshape(groups, blocks, rows, width)
    added = lax.dynamic_index_in_dim(parts, group, 0, keepdims=False).astype(jnp.float32)
    for shift in range(1, groups):
        piece = lax.dynamic_index_in_dim(parts, (group + shift) % groups, 0, keepdims=False)
        pairs = [(source, (source + shift) % groups) for source in range(groups)]
        added = added + lax.ppermute(piece, "dp", pairs).astype(jnp.float32)
    grad = added.astype(jnp.bfloat16)

    members = [[2 * chip + side for chip in range(chips)] for side in range(2)]

    def exchange(value):
        return lax.all_to_all(value, "owner", 0, 0, axis_index_groups=members, tiled=True)

    mine = exchange(grad)
    other = lax.ppermute(mine, "owner", swap)

    vmem = pl.BlockSpec(memory_space=pltpu.VMEM)
    smem = pl.BlockSpec(memory_space=pltpu.SMEM)
    square = (width, width)
    whole, portion = pl.pallas_call(
        product_kernel,
        out_shape=(
            jax.ShapeDtypeStruct(square, jnp.bfloat16),
            jax.ShapeDtypeStruct((chips * rows, width), jnp.bfloat16),
        ),
        in_specs=[smem, vmem, vmem, vmem, vmem],
        out_specs=(vmem, vmem),
        name="product",
    )(core[None].astype(jnp.int32), mine, other, roots[0], partner)
    update = exchange(portion.reshape(chips, rows, width))

    fresh, chosen = pl.pallas_call(
        root_kernel,
        out_shape=(
            jax.ShapeDtypeStruct(square, jnp.float32),
            jax.ShapeDtypeStruct(square, jnp.bfloat16),
        ),
        in_specs=[smem, vmem, vmem, vmem],
        out_specs=(vmem, vmem),
        scratch_shapes=[
            pltpu.VMEM(square, jnp.float32),
            pltpu.VMEM(square, jnp.float32),
            pltpu.VMEM(square, jnp.float32),
            pltpu.VMEM(square, jnp.bfloat16),
            pltpu.VMEM(square, jnp.bfloat16),
        ],
        name="root",
    )(jnp.stack([core, flag]).astype(jnp.int32), whole, stats[0], roots[0])
    return (fresh[None], chosen[None], update)


def solution(mesh):
    return jax.shard_map(
        local,
        mesh=mesh,
        in_specs=(
            P("dp", None, "owner", None),
            P(("dp", "owner"), None, None),
            P(("dp", "owner"), None, None),
            P("dp"),
        ),
        out_specs=(
            P(("dp", "owner"), None, None),
            P(("dp", "owner"), None, None),
            P("dp", "owner", None),
        ),
        check_vma=False,
    )
```

time: 105 us -> 46.9 us (0.45)
  matrix products: 37.4 us -> 0 us
  waiting for transfers between devices: 32.4 us -> 16 us
  between operations: 15.6 us -> 0.71 us
  Pallas kernels: 0 us -> 11.9 us
  local copies, waits for them, and re-layouts: 5.97 us -> 3.67 us
  starting transfers between devices: 10.6 us -> 12.6 us
    dot_general x19 -> x0, matrix products: 37.4 us -> none  [the longest x5 11.3 us: inverse_root(): result = jnp.dot(result, factor, precision=lax.Precision.HIGHEST)]
    reduce_scatter x1 -> x0, waiting for transfers between devices: 19.7 us -> none  [local(): lax.psum_scatter(grad_parts, 'dp', scatter_dimension=1, tiled=True)]
    pallas_call x0 -> x2, Pallas kernels: none -> 11.9 us  [the longest x1 9.12 us: local(): pl.pallas_call(root_kernel, out_shape=(jax.ShapeDtypeStruct(square, jnp.f...]
    ppermute x1 -> x3, waiting for transfers between devices: 0.01 us -> 7.82 us  [the longest x1 6.3 us: local(): added = added + lax.ppermute(piece, 'dp', pairs).astype(jnp.float32)]
    all_to_all x2, waiting for transfers between devices: 12 us -> 8.15 us  [exchange(): lax.all_to_all(value, 'owner', 0, 0, axis_index_groups=members, tiled=True)]
    ppermute x1 -> x3, starting transfers between devices: 0.41 us -> 3.13 us  [the longest x1 3.06 us: local(): added = added + lax.ppermute(piece, 'dp', pairs).astype(jnp.float32)]
    unnamed x1 -> x0, other arithmetic: 2.21 us -> none
    broadcast_in_dim x2 -> x0, local copies, waits for them, and re-layouts: 2.2 us -> none  [the longest x1 1.79 us: local(): doubled = jnp.repeat(grad, 2, axis=0)]
  transfers between devices with their start and end apart: 4 -> 5, of which waited for: 2 -> 3; matrix products, arithmetic and copies ran while one was open for 35% -> 4% of each run, Pallas kernels for 0% -> 19%
where the time goes in v1:
time: 46.9 us
  waiting for transfers between devices  16 us (34%)
  starting transfers between devices  12.6 us (27%)
  Pallas kernels  11.9 us (25%)
  local copies, waits for them, and re-layouts  3.67 us (8%)
  other arithmetic  2.08 us (4%)
  between operations  0.71 us (2%)
    all_to_all x2, starting transfers between devices, exchange(): lax.all_to_all(value, 'owner', 0, 0, axis_index_groups=members, tiled=True)  9.45 us
    pallas_call x1, Pallas kernels, local(): pl.pallas_call(root_kernel, out_shape=(jax.ShapeDtypeStruct(square, jnp.f...  9.12 us
    all_to_all x2, waiting for transfers between devices, exchange(): lax.all_to_all(value, 'owner', 0, 0, axis_index_groups=members, tiled=True)  8.15 us
    ppermute x1, waiting for transfers between devices, local(): added = added + lax.ppermute(piece, 'dp', pairs).astype(jnp.float32)  6.3 us
    ppermute x1, starting transfers between devices, local(): added = added + lax.ppermute(piece, 'dp', pairs).astype(jnp.float32)  3.06 us
    pallas_call x1, Pallas kernels, local(): pl.pallas_call(product_kernel, out_shape=(jax.ShapeDtypeStruct(square, jn...  2.79 us
    unnamed x13, local copies, waits for them, and re-layouts  2.07 us
    ppermute x1, waiting for transfers between devices, local(): other = lax.ppermute(mine, 'owner', swap)  1.51 us
  transfers between devices with their start and end apart: 5, of which 3 were waited for; matrix products, arithmetic and copies ran while one was open for 4% of the time, Pallas kernels for 19%

profile of v1, /device:TPU:0, one launch (start us, length us, event | category | flops | bytes accessed | tf_op | source)
XLA Modules:
  0.0 46.9 jit_solution(12686594786897046618)
XLA Ops:
  0.6 0.0 copy-start.2
  0.7 1.0 %dynamic-slice_bitcast_fusion = bf16[8,32,512]{2,1,0:T(8,128)(2,1)S(1)} fusion(bf16[2,8,32,512]{3,2,1,0:T(8,128)(2,1)} %bitcast.16, s32[]{:T(128)S(6)} %select_n.31), kind=kLoop, calls=%fused_computation.2 | loop fusion | bytes 524292 | tf_op jit(solution)/shard_map/jit(dynamic_index_in_dim)/squeeze | solution.py:110
  1.7 3.1 %collective-permute-start = (bf16[8,32,512]{2,1,0:T(8,128)(2,1)S(1)}, bf16[8,32,512]{2,1,0:T(8,128)(2,1)S(1)}, u32[]{:S(2)}, u32[]{:S(2)}) collective-permute-start(bf16[8,32,512]{2,1,0:T(8,128)(2,1)S(1)} %dynamic-slice_bitcast_fusion), channel_id=1, source_target_pairs={{0,16},{16,0},{1,17},{17,1},{2,18},{18,2},{3,19},{19,3},{4,20},{20... | collective-permute-start | bytes 786440 | tf_op jit(solution)/shard_map/ppermute | solution.py:112
  4.7 0.0 copy-start
  4.8 6.3 %collective-permute-done = bf16[8,32,512]{2,1,0:T(8,128)(2,1)S(1)} collective-permute-done((bf16[8,32,512]{2,1,0:T(8,128)(2,1)S(1)}, bf16[8,32,512]{2,1,0:T(8,128)(2,1)S(1)}, u32[]{:S(2)}, u32[]{:S(2)}) %collective-permute-start) | collective-permute-done | bytes 262176 | tf_op jit(solution)/shard_map/ppermute | solution.py:112
  11.1 0.0 copy-done.2
  11.1 0.8 %fusion = bf16[8,32,512]{2,1,0:T(8,128)(2,1)} fusion(bf16[8,32,512]{2,1,0:T(8,128)(2,1)S(1)} %collective-permute-done, bf16[2,8,32,512]{3,2,1,0:T(8,128)(2,1)S(1)} %bitcast.17, s32[]{:T(128)S(6)} %select_n.29), kind=kLoop, calls=%fused_computation.1 | loop fusion | flops 524288 | bytes 786436 | tf_op jit(solution)/shard_map/convert_element_type | solution.py:113
  11.8 6.0 %all-to-all-start = ((bf16[8,32,512]{2,1,0:T(8,128)(2,1)}), bf16[8,32,512]{2,1,0:T(8,128)(2,1)S(1)}, u32[]{:S(2)}, u32[]{:S(2)}) async-start(bf16[8,32,512]{2,1,0:T(8,128)(2,1)} %fusion), calls=%async_computation | async-start | bytes 524288 | tf_op jit(solution)/shard_map/all_to_all | solution.py:118
  17.9 0.0 copy-done
  17.9 0.1 collective-permute-start.2
  17.9 8.1 %all-to-all-done.mine = bf16[8,32,512]{2,1,0:T(8,128)(2,1)S(1)} async-done(((bf16[8,32,512]{2,1,0:T(8,128)(2,1)}), bf16[8,32,512]{2,1,0:T(8,128)(2,1)S(1)}, u32[]{:S(2)}, u32[]{:S(2)}) %all-to-all-start) | async-done | bytes 262176 | tf_op jit(solution)/shard_map/all_to_all | solution.py:118
  26.1 0.0 copy-start.1
  26.1 0.0 collective-permute-start.1
  26.1 0.0 collective-permute-done.2.partner
  26.1 0.0 copy-start.3
  26.1 1.5 %collective-permute-done.1.other = bf16[8,32,512]{2,1,0:T(8,128)(2,1)S(1)} collective-permute-done((bf16[8,32,512]{2,1,0:T(8,128)(2,1)S(1)}, bf16[8,32,512]{2,1,0:T(8,128)(2,1)S(1)}, u32[]{:S(2)}, u32[]{:S(2)}) %collective-permute-start.1) | collective-permute-done | bytes 262176 | tf_op jit(solution)/shard_map/ppermute | solution.py:121
  27.6 0.0 copy-start.4
  27.6 0.0 copy-done.1
  27.6 0.0 copy-done.3
  27.6 0.7 %copy-done.4 = bf16[8,32,512]{2,1,0:T(8,128)(2,1)} copy-done((bf16[8,32,512]{2,1,0:T(8,128)(2,1)}, bf16[8,32,512]{2,1,0:T(8,128)(2,1)S(1)}, u32[]{:S(2)}) %copy-start.4) | copy-done | bytes 262168
  28.3 2.8 %product.1 = (bf16[512,512]{1,0:T(8,128)(2,1)}, bf16[256,512]{1,0:T(8,128)(2,1)}) custom-call(s32[1]{0:T(128)} %bitcast.core, bf16[8,32,512]{2,1,0:T(8,128)(2,1)} %copy-done.1, bf16[8,32,512]{2,1,0:T(8,128)(2,1)} %copy-done.4, bf16[512,512]{1,0:T(8,128)(2,1)} %bitcast.12, bf16[512,512]{1,0:T(8,128)(2,1)} %copy-done.3), custom_call_target="tpu_custom_call" | custom-call | tf_op jit(solution)/shard_map/product/pallas_call | solution.py:126
  31.1 3.4 %all-to-all-start.1 = ((bf16[8,32,512]{2,1,0:T(8,128)(2,1)}), bf16[8,32,512]{2,1,0:T(8,128)(2,1)S(1)}, u32[]{:S(2)}, u32[]{:S(2)}) async-start(bf16[8,32,512]{2,1,0:T(8,128)(2,1)} %bitcast.18), calls=%async_computation.1 | async-start | bytes 524288 | tf_op jit(solution)/shard_map/all_to_all | solution.py:118
  34.6 0.0 copy-start.5
  34.6 0.6 %copy-done.5 = s32[8]{0:T(128)S(1)} copy-done((s32[8]{0:T(128)S(1)}, s32[8]{0:T(128)}, u32[]{:S(2)}) %copy-start.5) | copy-done | bytes 56
  35.2 0.6 %dynamic_slice.11 = s32[1]{0:T(128)} dynamic-slice(s32[8]{0:T(128)S(1)} %copy-done.5, s32[]{:T(128)S(6)} %select_n.28), dynamic_slice_sizes={1} | dynamic-slice | bytes 12 | tf_op jit(solution)/shard_map/jit(dynamic_index_in_dim)/dynamic_slice | solution.py:103
  35.8 1.3 %pad_add_fusion.flags = s32[2]{0:T(128)} fusion(s32[1]{0:T(128)} %dynamic_slice.11, s32[1]{0:T(128)} %bitcast.core), kind=kLoop, calls=%fused_computation.3 | loop fusion | flops 2 | bytes 16 | tf_op jit(solution)/shard_map/stack | solution.py:154
  37.1 9.1 %root.1 = (f32[512,512]{1,0:T(8,128)}, bf16[512,512]{1,0:T(8,128)(2,1)}) custom-call(s32[2]{0:T(128)} %pad_add_fusion.flags, bf16[512,512]{1,0:T(8,128)(2,1)} %get-tuple-element.7.whole, f32[512,512]{1,0:T(8,128)} %bitcast.15, bf16[512,512]{1,0:T(8,128)(2,1)} %bitcast.13), custom_call_target="tpu_custom_call" | custom-call | tf_op jit(solution)/shard_map/root/pallas_call | solution.py:138
  46.2 0.0 all-to-all-done.1
  46.2 0.7 %copy.8 = bf16[8,32,512]{2,1,0:T(8,128)(2,1)} copy(bf16[8,32,512]{2,1,0:T(8,128)(2,1)S(1)} %all-to-all-done.1) | data formatting | bytes 524288
Async XLA Ops:
  0.6 10.4 %copy-start.2 = (bf16[1,16,32,512]{3,2,1,0:T(8,128)(2,1)S(1)}, bf16[1,16,32,512]{3,2,1,0:T(8,128)(2,1)}, u32[]{:S(2)}) copy-start(bf16[1,16,32,512]{3,2,1,0:T(8,128)(2,1)} %param.4) | copy-start | bytes 1572868
  1.7 9.4 %collective-permute-start = (bf16[8,32,512]{2,1,0:T(8,128)(2,1)S(1)}, bf16[8,32,512]{2,1,0:T(8,128)(2,1)S(1)}, u32[]{:S(2)}, u32[]{:S(2)}) collective-permute-start(bf16[8,32,512]{2,1,0:T(8,128)(2,1)S(1)} %dynamic-slice_bitcast_fusion), channel_id=1, source_target_pairs={{0,16},{16,0},{1,17},{17,1},{2,18},{18,2},{3,19},{19,3},{4,20},{20... | collective-permute-start | bytes 786440 | tf_op jit(solution)/shard_map/ppermute | solution.py:112
  4.7 13.1 %copy-start = (bf16[1,512,512]{2,1,0:T(8,128)(2,1)S(1)}, bf16[1,512,512]{2,1,0:T(8,128)(2,1)}, u32[]{:S(2)}) copy-start(bf16[1,512,512]{2,1,0:T(8,128)(2,1)} %param.6) | copy-start | bytes 1572868
  11.8 14.3 %all-to-all-start = ((bf16[8,32,512]{2,1,0:T(8,128)(2,1)}), bf16[8,32,512]{2,1,0:T(8,128)(2,1)S(1)}, u32[]{:S(2)}, u32[]{:S(2)}) async-start(bf16[8,32,512]{2,1,0:T(8,128)(2,1)} %fusion), calls=%async_computation | async-start | bytes 524288 | tf_op jit(solution)/shard_map/all_to_all | solution.py:118
  17.9 8.2 %collective-permute-start.2 = (bf16[512,512]{1,0:T(8,128)(2,1)S(1)}, bf16[512,512]{1,0:T(8,128)(2,1)S(1)}, u32[]{:S(2)}, u32[]{:S(2)}) collective-permute-start(bf16[512,512]{1,0:T(8,128)(2,1)S(1)} %bitcast.14), channel_id=1, source_target_pairs={{0,1},{1,0},{2,3},{3,2},{4,5},{5,4},{6,7},{7,6},{8,9},{9,8},{10,11... | collective-permute-start | bytes 1572872 | tf_op jit(solution)/shard_map/ppermute | solution.py:105
  26.1 1.5 %copy-start.1 = (bf16[8,32,512]{2,1,0:T(8,128)(2,1)}, bf16[8,32,512]{2,1,0:T(8,128)(2,1)S(1)}, u32[]{:S(2)}) copy-start(bf16[8,32,512]{2,1,0:T(8,128)(2,1)S(1)} %all-to-all-done.mine) | copy-start | bytes 786436
  26.1 1.5 %collective-permute-start.1 = (bf16[8,32,512]{2,1,0:T(8,128)(2,1)S(1)}, bf16[8,32,512]{2,1,0:T(8,128)(2,1)S(1)}, u32[]{:S(2)}, u32[]{:S(2)}) collective-permute-start(bf16[8,32,512]{2,1,0:T(8,128)(2,1)S(1)} %all-to-all-done.mine), channel_id=1, source_target_pairs={{0,1},{1,0},{2,3},{3,2},{4,5},{5,4},{6,7},{7,6},{8,9},{9,8},{10,11... | collective-permute-start | bytes 786440 | tf_op jit(solution)/shard_map/ppermute | solution.py:121
  26.1 1.5 %copy-start.3 = (bf16[512,512]{1,0:T(8,128)(2,1)}, bf16[512,512]{1,0:T(8,128)(2,1)S(1)}, u32[]{:S(2)}) copy-start(bf16[512,512]{1,0:T(8,128)(2,1)S(1)} %collective-permute-done.2.partner) | copy-start | bytes 1572868
  27.6 0.7 %copy-start.4 = (bf16[8,32,512]{2,1,0:T(8,128)(2,1)}, bf16[8,32,512]{2,1,0:T(8,128)(2,1)S(1)}, u32[]{:S(2)}) copy-start(bf16[8,32,512]{2,1,0:T(8,128)(2,1)S(1)} %collective-permute-done.1.other) | copy-start | bytes 786436
  31.1 15.1 %all-to-all-start.1 = ((bf16[8,32,512]{2,1,0:T(8,128)(2,1)}), bf16[8,32,512]{2,1,0:T(8,128)(2,1)S(1)}, u32[]{:S(2)}, u32[]{:S(2)}) async-start(bf16[8,32,512]{2,1,0:T(8,128)(2,1)} %bitcast.18), calls=%async_computation.1 | async-start | bytes 524288 | tf_op jit(solution)/shard_map/all_to_all | solution.py:118
  34.6 0.7 %copy-start.5 = (s32[8]{0:T(128)S(1)}, s32[8]{0:T(128)}, u32[]{:S(2)}) copy-start(s32[8]{0:T(128)} %param.7) | copy-start | bytes 100

commit v2 on v1

--- a/solution.py
+++ b/solution.py
@@ -7,18 +7,27 @@
 
 ITERS = 5
 BETA = 0.8
+VMEM = pl.BlockSpec(memory_space=pltpu.VMEM)
+SMEM = pl.BlockSpec(memory_space=pltpu.SMEM)
+PARAMS = pltpu.CompilerParams(vmem_limit_bytes=16 * 2**20)
 
 
 def dot(a, b, dims=((1,), (0,))):
     return lax.dot_general(a, b, (dims, ((), ())), preferred_element_type=jnp.float32)
 
 
-def product_kernel(core, mine, other, root, partner, whole, portion):
-    @pl.when(core[0] == 0)
+def add_kernel(terms, out):
+    out[...] = (terms[0].astype(jnp.float32) + terms[1].astype(jnp.float32)).astype(jnp.bfloat16)
+
+
+def product_kernel(mine, other, root, partner, whole, portion):
+    side = lax.axis_index("owner") % 2
+
+    @pl.when(side == 0)
     def _():
         run_side(0, mine, other, root, partner, whole, portion)
 
-    @pl.when(core[0] == 1)
+    @pl.when(side == 1)
     def _():
         run_side(1, other, mine, partner, root, whole, portion)
 
@@ -38,16 +47,18 @@
 def root_kernel(flags, whole, stats, root, fresh, chosen, n, y, t, nb, yb):
     width = whole.shape[0]
     weight = (1.0 - BETA) / width
+    owner = lax.axis_index("owner")
+    flag = flags[owner // 2]
 
-    @pl.when(flags[0] == 0)
+    @pl.when(owner % 2 == 0)
     def _():
         fresh[...] = BETA * stats[...] + weight * dot(whole[...], whole[...], ((1,), (1,)))
 
-    @pl.when(flags[0] == 1)
+    @pl.when(owner % 2 == 1)
     def _():
         fresh[...] = BETA * stats[...] + weight * dot(whole[...], whole[...], ((0,), (0,)))
 
-    @pl.when(flags[1] == 1)
+    @pl.when(flag == 1)
     def _():
         value = fresh[...]
         total = jnp.sum(jnp.sum(value * value, axis=0, keepdims=True), axis=1, keepdims=True) + 1e-06
@@ -57,13 +68,10 @@
         nb[...] = start.astype(jnp.bfloat16)
         yb[...] = (-start).astype(jnp.bfloat16)
 
-        def square_step():
+        def advance(grown, first):
             t[...] = dot(nb[...], nb[...]) - 2.5 * n[...]
             low = t[...].astype(jnp.bfloat16)
-            return (dot(low, low) + 3.125 * t[...]).astype(jnp.bfloat16)
-
-        def advance(grown, first):
-            fourth = square_step()
+            fourth = (dot(low, low) + 3.125 * t[...]).astype(jnp.bfloat16)
             old = nb[...]
             if not first:
                 move = 1.25 * y[...] - grown * n[...] - dot(yb[...], old)
@@ -86,7 +94,7 @@
         scale = lax.rsqrt(jnp.sqrt(jnp.sqrt(total)))
         chosen[...] = ((last + jnp.where(diagonal, 1.25 * grown, 0.0)) * scale).astype(jnp.bfloat16)
 
-    @pl.when(flags[1] != 1)
+    @pl.when(flag != 1)
     def _():
         chosen[...] = root[...]
 
@@ -98,30 +106,38 @@
     _, total, rows, width = grad_parts.shape
     blocks = total // groups
     group = lax.axis_index("dp")
-    owner = lax.axis_index("owner")
-    core = owner % 2
-    flag = lax.dynamic_index_in_dim(refresh, owner // 2, 0, keepdims=False)
     swap = [(source, source ^ 1) for source in range(owners)]
     partner = lax.ppermute(roots[0], "owner", swap)
 
-    parts = grad_parts.reshape(groups, blocks, rows, width)
-    added = lax.dynamic_index_in_dim(parts, group, 0, keepdims=False).astype(jnp.float32)
-    for shift in range(1, groups):
-        piece = lax.dynamic_index_in_dim(parts, (group + shift) % groups, 0, keepdims=False)
-        pairs = [(source, (source + shift) % groups) for source in range(groups)]
-        added = added + lax.ppermute(piece, "dp", pairs).astype(jnp.float32)
-    grad = added.astype(jnp.bfloat16)
-
-    members = [[2 * chip + side for chip in range(chips)] for side in range(2)]
+    sides = range(2)
+    members = [[2 * chip + side for chip in range(chips)] for side in sides]
 
     def exchange(value):
         return lax.all_to_all(value, "owner", 0, 0, axis_index_groups=members, tiled=True)
 
-    mine = exchange(grad)
+    if groups == 2:
+        spread = [[pair * owners + one for pair in range(groups) for one in each] for each in members]
+        terms = lax.all_to_all(
+            grad_parts[0], ("dp", "owner"), 0, 0, axis_index_groups=spread, tiled=True
+        ).reshape(groups, chips, rows, width)
+        mine = pl.pallas_call(
+            add_kernel,
+            out_shape=jax.ShapeDtypeStruct((chips, rows, width), jnp.bfloat16),
+            in_specs=[VMEM],
+            out_specs=VMEM,
+            compiler_params=PARAMS,
+            name="add",
+        )(terms)
+    else:
+        parts = grad_parts.reshape(groups, blocks, rows, width)
+        added = lax.dynamic_index_in_dim(parts, group, 0, keepdims=False).astype(jnp.float32)
+        for shift in range(1, groups):
+            piece = lax.dynamic_index_in_dim(parts, (group + shift) % groups, 0, keepdims=False)
+            pairs = [(source, (source + shift) % groups) for source in range(groups)]
+            added = added + lax.ppermute(piece, "dp", pairs).astype(jnp.float32)
+        mine = exchange(added.astype(jnp.bfloat16))
     other = lax.ppermute(mine, "owner", swap)
 
-    vmem = pl.BlockSpec(memory_space=pltpu.VMEM)
-    smem = pl.BlockSpec(memory_space=pltpu.SMEM)
     square = (width, width)
     whole, portion = pl.pallas_call(
         product_kernel,
@@ -129,10 +145,11 @@
             jax.ShapeDtypeStruct(square, jnp.bfloat16),
             jax.ShapeDtypeStruct((chips * rows, width), jnp.bfloat16),
         ),
-        in_specs=[smem, vmem, vmem, vmem, vmem],
-        out_specs=(vmem, vmem),
+        in_specs=[VMEM, VMEM, VMEM, VMEM],
+        out_specs=(VMEM, VMEM),
+        compiler_params=PARAMS,
         name="product",
-    )(core[None].astype(jnp.int32), mine, other, roots[0], partner)
+    )(mine, other, roots[0], partner)
     update = exchange(portion.reshape(chips, rows, width))
 
     fresh, chosen = pl.pallas_call(
@@ -141,8 +158,8 @@
             jax.ShapeDtypeStruct(square, jnp.float32),
             jax.ShapeDtypeStruct(square, jnp.bfloat16),
         ),
-        in_specs=[smem, vmem, vmem, vmem],
-        out_specs=(vmem, vmem),
+        in_specs=[SMEM, VMEM, VMEM, VMEM],
+        out_specs=(VMEM, VMEM),
         scratch_shapes=[
             pltpu.VMEM(square, jnp.float32),
             pltpu.VMEM(square, jnp.float32),
@@ -150,8 +167,9 @@
             pltpu.VMEM(square, jnp.bfloat16),
             pltpu.VMEM(square, jnp.bfloat16),
         ],
+        compiler_params=PARAMS,
         name="root",
-    )(jnp.stack([core, flag]).astype(jnp.int32), whole, stats[0], roots[0])
+    )(refresh, whole, stats[0], roots[0])
     return (fresh[None], chosen[None], update)
 
 

time: 46.9 us -> 41.1 us (0.88)
  Pallas kernels: 11.9 us -> 3.5 us
  waiting for transfers between devices: 16 us -> 23.1 us
  local copies, waits for them, and re-layouts: 3.67 us -> 1.36 us
  other arithmetic: 2.08 us -> 0 us
  starting transfers between devices: 12.6 us -> 12.1 us
    all_to_all x0 -> x1, waiting for transfers between devices: none -> 15 us  [local(): lax.all_to_all(grad_parts[0], ('dp', 'owner'), 0, 0, axis_index_groups=sp...]
    all_to_all x0 -> x1, starting transfers between devices: none -> 8.48 us  [local(): lax.all_to_all(grad_parts[0], ('dp', 'owner'), 0, 0, axis_index_groups=sp...]
    pallas_call x1, Pallas kernels: 9.12 us -> 2.22 us  [local(): pl.pallas_call(root_kernel, out_shape=(jax.ShapeDtypeStruct(square, jnp.f...]
    ppermute x1 -> x0, waiting for transfers between devices: 6.3 us -> none  [local(): added = added + lax.ppermute(piece, 'dp', pairs).astype(jnp.float32)]
    all_to_all x2 -> x1, starting transfers between devices: 9.45 us -> 3.43 us  [exchange(): lax.all_to_all(value, 'owner', 0, 0, axis_index_groups=members, tiled=True)]
    ppermute x1 -> x0, starting transfers between devices: 3.06 us -> none  [local(): added = added + lax.ppermute(piece, 'dp', pairs).astype(jnp.float32)]
    all_to_all x2 -> x1, waiting for transfers between devices: 8.15 us -> 6.55 us  [exchange(): lax.all_to_all(value, 'owner', 0, 0, axis_index_groups=members, tiled=True)]
    pallas_call x1, Pallas kernels: 2.79 us -> 1.22 us  [local(): pl.pallas_call(product_kernel, out_shape=(jax.ShapeDtypeStruct(square, jn...]
  transfers between devices with their start and end apart: 5 -> 4, of which waited for: 3 -> 3; matrix products, arithmetic and copies ran while one was open for 4% -> 0% of each run, Pallas kernels for 19% -> 6%
where the time goes in v2:
time: 41.1 us; the launch traced here: 40.7 us
  waiting for transfers between devices  23.1 us (56%)
  starting transfers between devices  12.1 us (29%)
  Pallas kernels  3.5 us (9%)
  local copies, waits for them, and re-layouts  1.36 us (3%)
  between operations  0.7 us (2%)
    all_to_all x1, waiting for transfers between devices, local(): lax.all_to_all(grad_parts[0], ('dp', 'owner'), 0, 0, axis_index_groups=sp...  15 us
    all_to_all x1, starting transfers between devices, local(): lax.all_to_all(grad_parts[0], ('dp', 'owner'), 0, 0, axis_index_groups=sp...  8.48 us
    all_to_all x1, waiting for transfers between devices, exchange(): lax.all_to_all(value, 'owner', 0, 0, axis_index_groups=members, tiled=True)  6.55 us
    all_to_all x1, starting transfers between devices, exchange(): lax.all_to_all(value, 'owner', 0, 0, axis_index_groups=members, tiled=True)  3.43 us
    pallas_call x1, Pallas kernels, local(): pl.pallas_call(root_kernel, out_shape=(jax.ShapeDtypeStruct(square, jnp.f...  2.22 us
    ppermute x1, waiting for transfers between devices, local(): other = lax.ppermute(mine, 'owner', swap)  1.51 us
    unnamed x7, local copies, waits for them, and re-layouts  1.36 us
    pallas_call x1, Pallas kernels, local(): pl.pallas_call(product_kernel, out_shape=(jax.ShapeDtypeStruct(square, jn...  1.22 us
  transfers between devices with their start and end apart: 4, of which 3 were waited for; matrix products, arithmetic and copies ran while one was open for 0% of the time, Pallas kernels for 6%

profile of v2, /device:TPU:0, one launch (start us, length us, event | category | flops | bytes accessed | tf_op | source)
XLA Modules:
  0.0 40.7 jit_solution(5079889311101857347)
XLA Ops:
  0.6 0.0 copy-start
  0.6 8.5 %all-to-all-start = ((bf16[16,32,512]{2,1,0:T(8,128)(2,1)}), bf16[16,32,512]{2,1,0:T(8,128)(2,1)S(1)}, u32[]{:S(2)}, u32[]{:S(2)}) async-start(bf16[16,32,512]{2,1,0:T(8,128)(2,1)} %bitcast.12), calls=%async_computation | async-start | bytes 1048576 | tf_op jit(solution)/shard_map/all_to_all | solution.py:120
  9.1 0.0 copy-done
  9.1 0.1 collective-permute-start.1
  9.2 15.0 %all-to-all-done = bf16[16,32,512]{2,1,0:T(8,128)(2,1)S(1)} async-done(((bf16[16,32,512]{2,1,0:T(8,128)(2,1)}), bf16[16,32,512]{2,1,0:T(8,128)(2,1)S(1)}, u32[]{:S(2)}, u32[]{:S(2)}) %all-to-all-start) | async-done | bytes 524320 | tf_op jit(solution)/shard_map/all_to_all | solution.py:120
  24.3 0.1 add.1.mine
  24.3 0.0 copy-start.1
  24.3 0.1 collective-permute-start
  24.4 0.0 collective-permute-done.1.partner
  24.4 1.5 %collective-permute-done.other = bf16[8,32,512]{2,1,0:T(8,128)(2,1)S(1)} collective-permute-done((bf16[8,32,512]{2,1,0:T(8,128)(2,1)S(1)}, bf16[8,32,512]{2,1,0:T(8,128)(2,1)S(1)}, u32[]{:S(2)}, u32[]{:S(2)}) %collective-permute-start) | collective-permute-done | bytes 262176 | tf_op jit(solution)/shard_map/ppermute | solution.py:139
  25.9 1.2 %product.1 = (bf16[512,512]{1,0:T(8,128)(2,1)S(1)}, bf16[256,512]{1,0:T(8,128)(2,1)}) custom-call(bf16[8,32,512]{2,1,0:T(8,128)(2,1)S(1)} %add.1.mine, bf16[8,32,512]{2,1,0:T(8,128)(2,1)S(1)} %collective-permute-done.other, bf16[512,512]{1,0:T(8,128)(2,1)S(1)} %bitcast.8, bf16[512,512]{1,0:T(8,128)(2,1)S(1)} %collective-permute-done.1.partner), custom_call_target="tpu_custom_call" | custom-call | tf_op jit(solution)/shard_map/product/pallas_call | solution.py:142
  27.2 3.4 %all-to-all-start.1 = ((bf16[8,32,512]{2,1,0:T(8,128)(2,1)}), bf16[8,32,512]{2,1,0:T(8,128)(2,1)S(1)}, u32[]{:S(2)}, u32[]{:S(2)}) async-start(bf16[8,32,512]{2,1,0:T(8,128)(2,1)} %bitcast.6), calls=%async_computation.1 | async-start | bytes 524288 | tf_op jit(solution)/shard_map/all_to_all | solution.py:116
  30.6 0.0 copy-start.2
  30.6 0.0 copy-done.1
  30.6 0.6 %copy-done.2 = s32[8]{0:T(128)S(1)} copy-done((s32[8]{0:T(128)S(1)}, s32[8]{0:T(128)}, u32[]{:S(2)}) %copy-start.2) | copy-done | bytes 56
  31.3 2.2 %root.1 = (f32[512,512]{1,0:T(8,128)}, bf16[512,512]{1,0:T(8,128)(2,1)}) custom-call(s32[8]{0:T(128)S(1)} %copy-done.2, bf16[512,512]{1,0:T(8,128)(2,1)S(1)} %get-tuple-element.7.whole, f32[512,512]{1,0:T(8,128)S(1)} %bitcast.11, bf16[512,512]{1,0:T(8,128)(2,1)S(1)} %bitcast.9), custom_call_target="tpu_custom_call" | custom-call | tf_op jit(solution)/shard_map/root/pallas_call | solution.py:155
  33.5 6.5 %all-to-all-done.1 = bf16[8,32,512]{2,1,0:T(8,128)(2,1)S(1)} async-done(((bf16[8,32,512]{2,1,0:T(8,128)(2,1)}), bf16[8,32,512]{2,1,0:T(8,128)(2,1)S(1)}, u32[]{:S(2)}, u32[]{:S(2)}) %all-to-all-start.1) | async-done | bytes 262176 | tf_op jit(solution)/shard_map/all_to_all | solution.py:116
  40.0 0.7 %copy.8 = bf16[8,32,512]{2,1,0:T(8,128)(2,1)} copy(bf16[8,32,512]{2,1,0:T(8,128)(2,1)S(1)} %all-to-all-done.1) | data formatting | bytes 524288
Async XLA Ops:
  0.6 8.5 %copy-start = (bf16[1,512,512]{2,1,0:T(8,128)(2,1)S(1)}, bf16[1,512,512]{2,1,0:T(8,128)(2,1)}, u32[]{:S(2)}) copy-start(bf16[1,512,512]{2,1,0:T(8,128)(2,1)} %param.6) | copy-start | bytes 1572868
  0.6 23.6 %all-to-all-start = ((bf16[16,32,512]{2,1,0:T(8,128)(2,1)}), bf16[16,32,512]{2,1,0:T(8,128)(2,1)S(1)}, u32[]{:S(2)}, u32[]{:S(2)}) async-start(bf16[16,32,512]{2,1,0:T(8,128)(2,1)} %bitcast.12), calls=%async_computation | async-start | bytes 1048576 | tf_op jit(solution)/shard_map/all_to_all | solution.py:120
  9.1 15.3 %collective-permute-start.1 = (bf16[512,512]{1,0:T(8,128)(2,1)S(1)}, bf16[512,512]{1,0:T(8,128)(2,1)S(1)}, u32[]{:S(2)}, u32[]{:S(2)}) collective-permute-start(bf16[512,512]{1,0:T(8,128)(2,1)S(1)} %bitcast.7), channel_id=1, source_target_pairs={{0,1},{1,0},{2,3},{3,2},{4,5},{5,4},{6,7},{7,6},{8,9},{9,8},{10,11... | collective-permute-start | bytes 1572872 | tf_op jit(solution)/shard_map/ppermute | solution.py:110
  24.3 6.3 %copy-start.1 = (f32[1,512,512]{2,1,0:T(8,128)S(1)}, f32[1,512,512]{2,1,0:T(8,128)}, u32[]{:S(2)}) copy-start(f32[1,512,512]{2,1,0:T(8,128)} %param.5) | copy-start | bytes 3145732
  24.3 1.6 %collective-permute-start = (bf16[8,32,512]{2,1,0:T(8,128)(2,1)S(1)}, bf16[8,32,512]{2,1,0:T(8,128)(2,1)S(1)}, u32[]{:S(2)}, u32[]{:S(2)}) collective-permute-start(bf16[8,32,512]{2,1,0:T(8,128)(2,1)S(1)} %add.1.mine), channel_id=1, source_target_pairs={{0,1},{1,0},{2,3},{3,2},{4,5},{5,4},{6,7},{7,6},{8,9},{9,8},{10,11... | collective-permute-start | bytes 786440 | tf_op jit(solution)/shard_map/ppermute | solution.py:139
  27.2 12.9 %all-to-all-start.1 = ((bf16[8,32,512]{2,1,0:T(8,128)(2,1)}), bf16[8,32,512]{2,1,0:T(8,128)(2,1)S(1)}, u32[]{:S(2)}, u32[]{:S(2)}) async-start(bf16[8,32,512]{2,1,0:T(8,128)(2,1)} %bitcast.6), calls=%async_computation.1 | async-start | bytes 524288 | tf_op jit(solution)/shard_map/all_to_all | solution.py:116
  30.6 0.7 %copy-start.2 = (s32[8]{0:T(128)S(1)}, s32[8]{0:T(128)}, u32[]{:S(2)}) copy-start(s32[8]{0:T(128)} %flags.1) | copy-start | bytes 100

commit v3 on v2

--- a/solution.py
+++ b/solution.py
@@ -7,8 +7,13 @@
 
 ITERS = 5
 BETA = 0.8
+
+
+def order(side, chips):
+    return [(step + side * (chips // 2)) % chips for step in range(chips)]
+
 VMEM = pl.BlockSpec(memory_space=pltpu.VMEM)
-SMEM = pl.BlockSpec(memory_space=pltpu.SMEM)
+HBM = pl.BlockSpec(memory_space=pltpu.HBM)
 PARAMS = pltpu.CompilerParams(vmem_limit_bytes=16 * 2**20)
 
 
@@ -20,7 +25,7 @@
     out[...] = (terms[0].astype(jnp.float32) + terms[1].astype(jnp.float32)).astype(jnp.bfloat16)
 
 
-def product_kernel(mine, other, root, partner, whole, portion):
+def product_kernel(mine, other, root, partner, refresh, whole, portion):
     side = lax.axis_index("owner") % 2
 
     @pl.when(side == 0)
@@ -38,25 +43,47 @@
         whole[pl.ds(2 * chip * rows, rows), :] = first[chip]
         whole[pl.ds((2 * chip + 1) * rows, rows), :] = second[chip]
     picked = jnp.concatenate(
-        [left[pl.ds((2 * chip + side) * rows, rows), :] for chip in range(chips)], axis=0
+        [left[pl.ds((2 * chip + side) * rows, rows), :] for chip in order(side, chips)], axis=0
     )
     product = dot(picked, whole[...]).astype(jnp.bfloat16)
     portion[...] = dot(product, right[...]).astype(jnp.bfloat16)
 
 
-def root_kernel(flags, whole, stats, root, fresh, chosen, n, y, t, nb, yb):
+def place_kernel(moved, update, sent):
+    chips = moved.shape[0]
+    for side in range(2):
+
+        @pl.when(lax.axis_index("owner") % 2 == side)
+        def _():
+            copies = [
+                pltpu.make_async_copy(moved.at[step], update.at[chip], sent.at[step])
+                for step, chip in enumerate(order(side, chips))
+            ]
+            for copy in copies:
+                copy.start()
+            for copy in copies:
+                copy.wait()
+
+
+def root_kernel(refresh, whole, stats, root, out, chosen, fresh, n, y, t, nb, yb, flags, sent):
     width = whole.shape[0]
     weight = (1.0 - BETA) / width
     owner = lax.axis_index("owner")
+    fetch = pltpu.make_async_copy(refresh, flags, sent.at[0])
+    fetch.start()
+
+    @pl.when(owner % 2 == 0)
+    def _():
+        fresh[...] = BETA * stats[...] + weight * dot(whole[...], whole[...], ((1,), (1,)))
+
+    @pl.when(owner % 2 == 1)
+    def _():
+        fresh[...] = BETA * stats[...] + weight * dot(whole[...], whole[...], ((0,), (0,)))
+
+    store = pltpu.make_async_copy(fresh, out, sent.at[1])
+    store.start()
+    fetch.wait()
     flag = flags[owner // 2]
-
-    @pl.when(owner % 2 == 0)
-    def _():
-        fresh[...] = BETA * stats[...] + weight * dot(whole[...], whole[...], ((1,), (1,)))
-
-    @pl.when(owner % 2 == 1)
-    def _():
-        fresh[...] = BETA * stats[...] + weight * dot(whole[...], whole[...], ((0,), (0,)))
 
     @pl.when(flag == 1)
     def _():
@@ -97,6 +124,8 @@
     @pl.when(flag != 1)
     def _():
         chosen[...] = root[...]
+
+    store.wait()
 
 
 def local(grad_parts, stats, roots, refresh):
@@ -145,12 +174,25 @@
             jax.ShapeDtypeStruct(square, jnp.bfloat16),
             jax.ShapeDtypeStruct((chips * rows, width), jnp.bfloat16),
         ),
-        in_specs=[VMEM, VMEM, VMEM, VMEM],
+        in_specs=[VMEM, VMEM, VMEM, VMEM, HBM],
         out_specs=(VMEM, VMEM),
         compiler_params=PARAMS,
         name="product",
-    )(mine, other, roots[0], partner)
-    update = exchange(portion.reshape(chips, rows, width))
+    )(mine, other, roots[0], partner, refresh)
+    shape = (chips, rows, width)
+    served = [[2 * chip + side for chip in order(side, chips)] for side in range(2)]
+    moved = lax.all_to_all(
+        portion.reshape(shape), "owner", 0, 0, axis_index_groups=served, tiled=True
+    )
+    update = pl.pallas_call(
+        place_kernel,
+        out_shape=jax.ShapeDtypeStruct(shape, jnp.bfloat16),
+        in_specs=[VMEM],
+        out_specs=HBM,
+        scratch_shapes=[pltpu.SemaphoreType.DMA((chips,))],
+        compiler_params=PARAMS,
+        name="place",
+    )(moved)
 
     fresh, chosen = pl.pallas_call(
         root_kernel,
@@ -158,14 +200,17 @@
             jax.ShapeDtypeStruct(square, jnp.float32),
             jax.ShapeDtypeStruct(square, jnp.bfloat16),
         ),
-        in_specs=[SMEM, VMEM, VMEM, VMEM],
-        out_specs=(VMEM, VMEM),
+        in_specs=[HBM, VMEM, VMEM, VMEM],
+        out_specs=(HBM, VMEM),
         scratch_shapes=[
+            pltpu.VMEM(square, jnp.float32),
             pltpu.VMEM(square, jnp.float32),
             pltpu.VMEM(square, jnp.float32),
             pltpu.VMEM(square, jnp.float32),
             pltpu.VMEM(square, jnp.bfloat16),
             pltpu.VMEM(square, jnp.bfloat16),
+            pltpu.SMEM(refresh.shape, jnp.int32),
+            pltpu.SemaphoreType.DMA((2,)),
         ],
         compiler_params=PARAMS,
         name="root",

time: 41.1 us -> 39.9 us (0.971)
  Pallas kernels: 3.5 us -> 9.37 us
  waiting for transfers between devices: 23.1 us -> 17.4 us
  local copies, waits for them, and re-layouts: 1.36 us -> 0.01 us
    all_to_all x1, waiting for transfers between devices: 6.55 us -> 0.88 us  [local(): lax.all_to_all(portion.reshape(shape), 'owner', 0, 0, axis_index_groups=s...]
    pallas_call x1, Pallas kernels: 2.22 us -> 7.33 us  [local(): pl.pallas_call(root_kernel, out_shape=(jax.ShapeDtypeStruct(square, jnp.f...]
    unnamed x7 -> x6, local copies, waits for them, and re-layouts: 1.36 us -> 0.01 us
    pallas_call x0 -> x1, Pallas kernels: none -> 0.76 us  [local(): pl.pallas_call(place_kernel, out_shape=jax.ShapeDtypeStruct(shape, jnp.bf...]
  transfers between devices with their start and end apart: 4 -> 4, of which waited for: 3 -> 3; matrix products, arithmetic and copies ran while one was open for 0% -> 0% of each run, Pallas kernels for 6% -> 19%
where the time goes in v3:
time: 39.9 us; the launch traced here: 39.6 us
  waiting for transfers between devices  17.4 us (44%)
  starting transfers between devices  12.1 us (30%)
  Pallas kernels  9.37 us (23%)
  between operations  0.7 us (2%)
    all_to_all x1, waiting for transfers between devices, local(): lax.all_to_all(grad_parts[0], ('dp', 'owner'), 0, 0, axis_index_groups=sp...  15 us
    all_to_all x1, starting transfers between devices, local(): lax.all_to_all(grad_parts[0], ('dp', 'owner'), 0, 0, axis_index_groups=sp...  8.48 us
    pallas_call x1, Pallas kernels, local(): pl.pallas_call(root_kernel, out_shape=(jax.ShapeDtypeStruct(square, jnp.f...  7.33 us
    all_to_all x1, starting transfers between devices, local(): lax.all_to_all(portion.reshape(shape), 'owner', 0, 0, axis_index_groups=s...  3.43 us
    ppermute x1, waiting for transfers between devices, local(): other = lax.ppermute(mine, 'owner', swap)  1.51 us
    pallas_call x1, Pallas kernels, local(): pl.pallas_call(product_kernel, out_shape=(jax.ShapeDtypeStruct(square, jn...  1.22 us
    all_to_all x1, waiting for transfers between devices, local(): lax.all_to_all(portion.reshape(shape), 'owner', 0, 0, axis_index_groups=s...  0.88 us
  transfers between devices with their start and end apart: 4, of which 3 were waited for; matrix products, arithmetic and copies ran while one was open for 0% of the time, Pallas kernels for 19%

profile of v3, /device:TPU:0, one launch (start us, length us, event | category | flops | bytes accessed | tf_op | source)
XLA Modules:
  0.0 39.6 jit_solution(345232589972523122)
XLA Ops:
  0.6 0.0 copy-start
  0.6 8.5 %all-to-all-start = ((bf16[16,32,512]{2,1,0:T(8,128)(2,1)}), bf16[16,32,512]{2,1,0:T(8,128)(2,1)S(1)}, u32[]{:S(2)}, u32[]{:S(2)}) async-start(bf16[16,32,512]{2,1,0:T(8,128)(2,1)} %bitcast.12), calls=%async_computation | async-start | bytes 1048576 | tf_op jit(solution)/shard_map/all_to_all | solution.py:149
  9.1 0.0 copy-done
  9.1 0.1 collective-permute-start.1
  9.2 15.0 %all-to-all-done = bf16[16,32,512]{2,1,0:T(8,128)(2,1)S(1)} async-done(((bf16[16,32,512]{2,1,0:T(8,128)(2,1)}), bf16[16,32,512]{2,1,0:T(8,128)(2,1)S(1)}, u32[]{:S(2)}, u32[]{:S(2)}) %all-to-all-start) | async-done | bytes 524320 | tf_op jit(solution)/shard_map/all_to_all | solution.py:149
  24.3 0.0 copy-start.2
  24.3 0.1 add.1.mine
  24.3 0.0 copy-start.1
  24.3 0.1 collective-permute-start
  24.4 0.0 collective-permute-done.1.partner
  24.4 1.5 %collective-permute-done.other = bf16[8,32,512]{2,1,0:T(8,128)(2,1)S(1)} collective-permute-done((bf16[8,32,512]{2,1,0:T(8,128)(2,1)S(1)}, bf16[8,32,512]{2,1,0:T(8,128)(2,1)S(1)}, u32[]{:S(2)}, u32[]{:S(2)}) %collective-permute-start) | collective-permute-done | bytes 262176 | tf_op jit(solution)/shard_map/ppermute | solution.py:168
  25.9 0.0 copy-done.2
  26.0 1.2 %product.1 = (bf16[512,512]{1,0:T(8,128)(2,1)S(1)}, bf16[256,512]{1,0:T(8,128)(2,1)}) custom-call(bf16[8,32,512]{2,1,0:T(8,128)(2,1)S(1)} %add.1.mine, bf16[8,32,512]{2,1,0:T(8,128)(2,1)S(1)} %collective-permute-done.other, bf16[512,512]{1,0:T(8,128)(2,1)S(1)} %bitcast.8, bf16[512,512]{1,0:T(8,128)(2,1)S(1)} %collective-permute-done.1.partner, s32[8]{0:T(128)S(1)} %copy-done.2), custom_call_target="tpu_custom_call" | custom-call | tf_op jit(solution)/shard_map/product/pallas_call | solution.py:171
  27.2 3.4 %all-to-all-start.1 = ((bf16[8,32,512]{2,1,0:T(8,128)(2,1)}), bf16[8,32,512]{2,1,0:T(8,128)(2,1)S(1)}, u32[]{:S(2)}, u32[]{:S(2)}) async-start(bf16[8,32,512]{2,1,0:T(8,128)(2,1)} %bitcast.6), calls=%async_computation.1 | async-start | bytes 524288 | tf_op jit(solution)/shard_map/all_to_all | solution.py:184
  30.6 0.0 copy-done.1
  30.6 7.3 %root.1 = (f32[512,512]{1,0:T(8,128)}, bf16[512,512]{1,0:T(8,128)(2,1)}) custom-call(s32[8]{0:T(128)S(1)} %copy-done.2, bf16[512,512]{1,0:T(8,128)(2,1)S(1)} %get-tuple-element.7.whole, f32[512,512]{1,0:T(8,128)S(1)} %bitcast.11, bf16[512,512]{1,0:T(8,128)(2,1)S(1)} %bitcast.9), custom_call_target="tpu_custom_call" | custom-call | tf_op jit(solution)/shard_map/root/pallas_call | solution.py:197
  38.0 0.9 %all-to-all-done.1.moved = bf16[8,32,512]{2,1,0:T(8,128)(2,1)S(1)} async-done(((bf16[8,32,512]{2,1,0:T(8,128)(2,1)}), bf16[8,32,512]{2,1,0:T(8,128)(2,1)S(1)}, u32[]{:S(2)}, u32[]{:S(2)}) %all-to-all-start.1) | async-done | bytes 262176 | tf_op jit(solution)/shard_map/all_to_all | solution.py:184
  38.8 0.8 %place.1 = bf16[8,32,512]{2,1,0:T(8,128)(2,1)} custom-call(bf16[8,32,512]{2,1,0:T(8,128)(2,1)S(1)} %all-to-all-done.1.moved), custom_call_target="tpu_custom_call" | custom-call | tf_op jit(solution)/shard_map/place/pallas_call | solution.py:187
Async XLA Ops:
  0.6 8.5 %copy-start = (bf16[1,512,512]{2,1,0:T(8,128)(2,1)S(1)}, bf16[1,512,512]{2,1,0:T(8,128)(2,1)}, u32[]{:S(2)}) copy-start(bf16[1,512,512]{2,1,0:T(8,128)(2,1)} %param.6) | copy-start | bytes 1572868
  0.6 23.6 %all-to-all-start = ((bf16[16,32,512]{2,1,0:T(8,128)(2,1)}), bf16[16,32,512]{2,1,0:T(8,128)(2,1)S(1)}, u32[]{:S(2)}, u32[]{:S(2)}) async-start(bf16[16,32,512]{2,1,0:T(8,128)(2,1)} %bitcast.12), calls=%async_computation | async-start | bytes 1048576 | tf_op jit(solution)/shard_map/all_to_all | solution.py:149
  9.1 15.3 %collective-permute-start.1 = (bf16[512,512]{1,0:T(8,128)(2,1)S(1)}, bf16[512,512]{1,0:T(8,128)(2,1)S(1)}, u32[]{:S(2)}, u32[]{:S(2)}) collective-permute-start(bf16[512,512]{1,0:T(8,128)(2,1)S(1)} %bitcast.7), channel_id=1, source_target_pairs={{0,1},{1,0},{2,3},{3,2},{4,5},{5,4},{6,7},{7,6},{8,9},{9,8},{10,11... | collective-permute-start | bytes 1572872 | tf_op jit(solution)/shard_map/ppermute | solution.py:139
  24.3 1.7 %copy-start.2 = (s32[8]{0:T(128)S(1)}, s32[8]{0:T(128)}, u32[]{:S(2)}) copy-start(s32[8]{0:T(128)} %refresh.3) | copy-start | bytes 100
  24.3 6.3 %copy-start.1 = (f32[1,512,512]{2,1,0:T(8,128)S(1)}, f32[1,512,512]{2,1,0:T(8,128)}, u32[]{:S(2)}) copy-start(f32[1,512,512]{2,1,0:T(8,128)} %param.5) | copy-start | bytes 3145732
  24.3 1.6 %collective-permute-start = (bf16[8,32,512]{2,1,0:T(8,128)(2,1)S(1)}, bf16[8,32,512]{2,1,0:T(8,128)(2,1)S(1)}, u32[]{:S(2)}, u32[]{:S(2)}) collective-permute-start(bf16[8,32,512]{2,1,0:T(8,128)(2,1)S(1)} %add.1.mine), channel_id=1, source_target_pairs={{0,1},{1,0},{2,3},{3,2},{4,5},{5,4},{6,7},{7,6},{8,9},{9,8},{10,11... | collective-permute-start | bytes 786440 | tf_op jit(solution)/shard_map/ppermute | solution.py:168
  27.2 11.7 %all-to-all-start.1 = ((bf16[8,32,512]{2,1,0:T(8,128)(2,1)}), bf16[8,32,512]{2,1,0:T(8,128)(2,1)S(1)}, u32[]{:S(2)}, u32[]{:S(2)}) async-start(bf16[8,32,512]{2,1,0:T(8,128)(2,1)} %bitcast.6), calls=%async_computation.1 | async-start | bytes 524288 | tf_op jit(solution)/shard_map/all_to_all | solution.py:184

commit v4 on v3

--- a/solution.py
+++ b/solution.py
@@ -10,7 +10,10 @@
 
 
 def order(side, chips):
-    return [(step + side * (chips // 2)) % chips for step in range(chips)]
+    half = chips // 2
+    return [
+        (turn ^ side) * half + (step + (turn * (1 - side)) * (half // 2)) % half for turn in range(2) for step in range(half)
+    ]
 
 VMEM = pl.BlockSpec(memory_space=pltpu.VMEM)
 HBM = pl.BlockSpec(memory_space=pltpu.HBM)

time: 39.9 us -> 39.7 us (level)
  Pallas kernels: 9.37 us -> 4.32 us
  waiting for transfers between devices: 17.4 us -> 22.2 us
    pallas_call x1, Pallas kernels: 7.33 us -> 2.28 us  [local(): pl.pallas_call(root_kernel, out_shape=(jax.ShapeDtypeStruct(square, jnp.f...]
    all_to_all x1, waiting for transfers between devices: 0.88 us -> 5.68 us  [local(): lax.all_to_all(portion.reshape(shape), 'owner', 0, 0, axis_index_groups=s...]
  transfers between devices with their start and end apart: 4 -> 4, of which waited for: 3 -> 3; matrix products, arithmetic and copies ran while one was open for 0% -> 0% of each run, Pallas kernels for 19% -> 6%
where the time goes in v4:
time: 39.7 us; the launch traced here: 39.3 us
  waiting for transfers between devices  22.2 us (56%)
  starting transfers between devices  12.1 us (30%)
  Pallas kernels  4.32 us (11%)
  between operations  0.7 us (2%)
    all_to_all x1, waiting for transfers between devices, local(): lax.all_to_all(grad_parts[0], ('dp', 'owner'), 0, 0, axis_index_groups=sp...  15 us
    all_to_all x1, starting transfers between devices, local(): lax.all_to_all(grad_parts[0], ('dp', 'owner'), 0, 0, axis_index_groups=sp...  8.48 us
    all_to_all x1, waiting for transfers between devices, local(): lax.all_to_all(portion.reshape(shape), 'owner', 0, 0, axis_index_groups=s...  5.68 us
    all_to_all x1, starting transfers between devices, local(): lax.all_to_all(portion.reshape(shape), 'owner', 0, 0, axis_index_groups=s...  3.43 us
    pallas_call x1, Pallas kernels, local(): pl.pallas_call(root_kernel, out_shape=(jax.ShapeDtypeStruct(square, jnp.f...  2.28 us
    ppermute x1, waiting for transfers between devices, local(): other = lax.ppermute(mine, 'owner', swap)  1.51 us
    pallas_call x1, Pallas kernels, local(): pl.pallas_call(product_kernel, out_shape=(jax.ShapeDtypeStruct(square, jn...  1.22 us
  transfers between devices with their start and end apart: 4, of which 3 were waited for; matrix products, arithmetic and copies ran while one was open for 0% of the time, Pallas kernels for 6%

profile of v4, /device:TPU:0, one launch (start us, length us, event | category | flops | bytes accessed | tf_op | source)
XLA Modules:
  0.0 39.3 jit_solution(2988685053197037530)
XLA Ops:
  0.6 0.0 copy-start
  0.6 8.5 %all-to-all-start = ((bf16[16,32,512]{2,1,0:T(8,128)(2,1)}), bf16[16,32,512]{2,1,0:T(8,128)(2,1)S(1)}, u32[]{:S(2)}, u32[]{:S(2)}) async-start(bf16[16,32,512]{2,1,0:T(8,128)(2,1)} %bitcast.12), calls=%async_computation | async-start | bytes 1048576 | tf_op jit(solution)/shard_map/all_to_all | solution.py:152
  9.1 0.0 copy-done
  9.1 0.1 collective-permute-start.1
  9.2 15.0 %all-to-all-done = bf16[16,32,512]{2,1,0:T(8,128)(2,1)S(1)} async-done(((bf16[16,32,512]{2,1,0:T(8,128)(2,1)}), bf16[16,32,512]{2,1,0:T(8,128)(2,1)S(1)}, u32[]{:S(2)}, u32[]{:S(2)}) %all-to-all-start) | async-done | bytes 524320 | tf_op jit(solution)/shard_map/all_to_all | solution.py:152
  24.3 0.0 copy-start.2
  24.3 0.1 add.1.mine
  24.3 0.0 copy-start.1
  24.3 0.1 collective-permute-start
  24.4 0.0 collective-permute-done.1.partner
  24.4 1.5 %collective-permute-done.other = bf16[8,32,512]{2,1,0:T(8,128)(2,1)S(1)} collective-permute-done((bf16[8,32,512]{2,1,0:T(8,128)(2,1)S(1)}, bf16[8,32,512]{2,1,0:T(8,128)(2,1)S(1)}, u32[]{:S(2)}, u32[]{:S(2)}) %collective-permute-start) | collective-permute-done | bytes 262176 | tf_op jit(solution)/shard_map/ppermute | solution.py:171
  25.9 0.0 copy-done.2
  26.0 1.2 %product.1 = (bf16[512,512]{1,0:T(8,128)(2,1)S(1)}, bf16[256,512]{1,0:T(8,128)(2,1)}) custom-call(bf16[8,32,512]{2,1,0:T(8,128)(2,1)S(1)} %add.1.mine, bf16[8,32,512]{2,1,0:T(8,128)(2,1)S(1)} %collective-permute-done.other, bf16[512,512]{1,0:T(8,128)(2,1)S(1)} %bitcast.8, bf16[512,512]{1,0:T(8,128)(2,1)S(1)} %collective-permute-done.1.partner, s32[8]{0:T(128)S(1)} %copy-done.2), custom_call_target="tpu_custom_call" | custom-call | tf_op jit(solution)/shard_map/product/pallas_call | solution.py:174
  27.2 3.4 %all-to-all-start.1 = ((bf16[8,32,512]{2,1,0:T(8,128)(2,1)}), bf16[8,32,512]{2,1,0:T(8,128)(2,1)S(1)}, u32[]{:S(2)}, u32[]{:S(2)}) async-start(bf16[8,32,512]{2,1,0:T(8,128)(2,1)} %bitcast.6), calls=%async_computation.1 | async-start | bytes 524288 | tf_op jit(solution)/shard_map/all_to_all | solution.py:187
  30.6 0.0 copy-done.1
  30.6 2.3 %root.1 = (f32[512,512]{1,0:T(8,128)}, bf16[512,512]{1,0:T(8,128)(2,1)}) custom-call(s32[8]{0:T(128)S(1)} %copy-done.2, bf16[512,512]{1,0:T(8,128)(2,1)S(1)} %get-tuple-element.7.whole, f32[512,512]{1,0:T(8,128)S(1)} %bitcast.11, bf16[512,512]{1,0:T(8,128)(2,1)S(1)} %bitcast.9), custom_call_target="tpu_custom_call" | custom-call | tf_op jit(solution)/shard_map/root/pallas_call | solution.py:200
  32.9 5.7 %all-to-all-done.1.moved = bf16[8,32,512]{2,1,0:T(8,128)(2,1)S(1)} async-done(((bf16[8,32,512]{2,1,0:T(8,128)(2,1)}), bf16[8,32,512]{2,1,0:T(8,128)(2,1)S(1)}, u32[]{:S(2)}, u32[]{:S(2)}) %all-to-all-start.1) | async-done | bytes 262176 | tf_op jit(solution)/shard_map/all_to_all | solution.py:187
  38.6 0.8 %place.1 = bf16[8,32,512]{2,1,0:T(8,128)(2,1)} custom-call(bf16[8,32,512]{2,1,0:T(8,128)(2,1)S(1)} %all-to-all-done.1.moved), custom_call_target="tpu_custom_call" | custom-call | tf_op jit(solution)/shard_map/place/pallas_call | solution.py:190
Async XLA Ops:
  0.6 8.5 %copy-start = (bf16[1,512,512]{2,1,0:T(8,128)(2,1)S(1)}, bf16[1,512,512]{2,1,0:T(8,128)(2,1)}, u32[]{:S(2)}) copy-start(bf16[1,512,512]{2,1,0:T(8,128)(2,1)} %param.6) | copy-start | bytes 1572868
  0.6 23.6 %all-to-all-start = ((bf16[16,32,512]{2,1,0:T(8,128)(2,1)}), bf16[16,32,512]{2,1,0:T(8,128)(2,1)S(1)}, u32[]{:S(2)}, u32[]{:S(2)}) async-start(bf16[16,32,512]{2,1,0:T(8,128)(2,1)} %bitcast.12), calls=%async_computation | async-start | bytes 1048576 | tf_op jit(solution)/shard_map/all_to_all | solution.py:152
  9.1 15.3 %collective-permute-start.1 = (bf16[512,512]{1,0:T(8,128)(2,1)S(1)}, bf16[512,512]{1,0:T(8,128)(2,1)S(1)}, u32[]{:S(2)}, u32[]{:S(2)}) collective-permute-start(bf16[512,512]{1,0:T(8,128)(2,1)S(1)} %bitcast.7), channel_id=1, source_target_pairs={{0,1},{1,0},{2,3},{3,2},{4,5},{5,4},{6,7},{7,6},{8,9},{9,8},{10,11... | collective-permute-start | bytes 1572872 | tf_op jit(solution)/shard_map/ppermute | solution.py:142
  24.3 1.7 %copy-start.2 = (s32[8]{0:T(128)S(1)}, s32[8]{0:T(128)}, u32[]{:S(2)}) copy-start(s32[8]{0:T(128)} %refresh.3) | copy-start | bytes 100
  24.3 6.3 %copy-start.1 = (f32[1,512,512]{2,1,0:T(8,128)S(1)}, f32[1,512,512]{2,1,0:T(8,128)}, u32[]{:S(2)}) copy-start(f32[1,512,512]{2,1,0:T(8,128)} %param.5) | copy-start | bytes 3145732
  24.3 1.6 %collective-permute-start = (bf16[8,32,512]{2,1,0:T(8,128)(2,1)S(1)}, bf16[8,32,512]{2,1,0:T(8,128)(2,1)S(1)}, u32[]{:S(2)}, u32[]{:S(2)}) collective-permute-start(bf16[8,32,512]{2,1,0:T(8,128)(2,1)S(1)} %add.1.mine), channel_id=1, source_target_pairs={{0,1},{1,0},{2,3},{3,2},{4,5},{5,4},{6,7},{7,6},{8,9},{9,8},{10,11... | collective-permute-start | bytes 786440 | tf_op jit(solution)/shard_map/ppermute | solution.py:171
  27.2 11.4 %all-to-all-start.1 = ((bf16[8,32,512]{2,1,0:T(8,128)(2,1)}), bf16[8,32,512]{2,1,0:T(8,128)(2,1)S(1)}, u32[]{:S(2)}, u32[]{:S(2)}) async-start(bf16[8,32,512]{2,1,0:T(8,128)(2,1)} %bitcast.6), calls=%async_computation.1 | async-start | bytes 524288 | tf_op jit(solution)/shard_map/all_to_all | solution.py:187
